TPU v7x, 32 devices: a whole 2x2x4 slice. The times are simulated.
32 devices in a mesh: groups: 2 (over y), dp: 4 (over x, core), tp: 4 (over z).
Axes of the slice: x: 2, y: 2, z: 4, core: 2. Of those that a mesh axis runs over, the one named last changes fastest.
Arguments:
- tokens: bfloat16 [256, 6144], P(('groups', 'tp'), 'dp'), parts along dimension 0, may hold values from -6 to 6
- gate_weight: bfloat16 [6144, 16384], P('dp', 'tp'), may hold values from -0.078125 to 0.078125
- up_weight: bfloat16 [6144, 16384], P('dp', 'tp'), may hold values from -0.078125 to 0.078125
- down_weight: bfloat16 [16384, 6144], P('tp', 'dp'), may hold values from -0.046875 to 0.046875
- expert_ids: int32 [256, 2], P(('groups', 'tp')), parts along dimension 0, may hold values from 0 to 7, as said below
- route_weights: float32 [256, 2], P(('groups', 'tp')), parts along dimension 0, may hold values from 0.1 to 1
Outputs:
- mixed: bfloat16 [256, 6144], P(('groups', 'tp'), 'dp'), parts along dimension 0
There are 2 independent parts, one for each index of `groups`. A program takes and returns all parts, laid end to end along the dimension named above; an argument that names none is the same for every part. Nothing has to cross between parts.
Inputs may be any that keep to these rules, and one draw needn't show every extreme that they name: `expert_ids`: each row names two different experts. Among the 32 rows of one index of tp, expert 0 is named by 1 to 16 rows, and by exactly 16 rows on at least one index of tp.
All inputs are finite; a program needn't handle non-finite values.
Results may differ from a plain program's by a relative error of at most 0.03.
Values may be sent and summed in bfloat16 or wider, within the bound.
No kernel may reach another device: no remote copies, remote signals or barrier semaphores. Data moves between devices by JAX's collectives and lax.ppermute only.
A program may use at most 64 MiB of HBM per device.

v0:
```python
import jax
import jax.numpy as jnp
from jax import lax
from jax.sharding import PartitionSpec as P

MOST = 16


def shards(tokens, gate_weight, up_weight, down_weight, expert_ids, route_weights):
    held_mask = expert_ids == 0
    combine = jnp.sum(jnp.where(held_mask, route_weights, jnp.zeros_like(route_weights)), axis=1)
    hidden_width = gate_weight.shape[1]
    routed = jnp.any(held_mask, axis=1)
    slot_rank = jnp.cumsum(routed.astype(jnp.int32)) - 1
    slot_ids = jnp.arange(MOST, dtype=jnp.int32)
    dispatch = ((slot_rank[None, :] == slot_ids[:, None]) & routed[None, :]).astype(jnp.bfloat16)
    packed = jnp.dot(dispatch, tokens, preferred_element_type=jnp.float32).astype(jnp.bfloat16)
    row_block = lax.all_gather(packed, "tp", axis=0, tiled=True)
    gate_part = jnp.dot(row_block, gate_weight, preferred_element_type=jnp.float32).astype(
        jnp.bfloat16
    )
    up_part = jnp.dot(row_block, up_weight, preferred_element_type=jnp.float32).astype(jnp.bfloat16)
    gate_up = jnp.concatenate([gate_part, up_part], axis=1)
    summed = lax.psum(gate_up, "dp").astype(jnp.float32)
    hidden = (jax.nn.silu(summed[:, :hidden_width]) * summed[:, hidden_width:]).astype(jnp.bfloat16)
    partial_value = jnp.dot(hidden, down_weight, preferred_element_type=jnp.float32)
    result = jnp.dot(
        dispatch.T.astype(jnp.float32),
        lax.psum_scatter(
            partial_value.astype(jnp.bfloat16), "tp", scatter_dimension=0, tiled=True
        ).astype(jnp.float32),
        precision=lax.Precision.HIGHEST,
    )
    return (combine[:, None] * result).astype(jnp.bfloat16)


def solution(mesh):
    in_specs = (
        P(("groups", "tp"), "dp"),
        P("dp", "tp"),
        P("dp", "tp"),
        P("tp", "dp"),
        P(("groups", "tp"), None),
        P(("groups", "tp"), None),
    )
    out_specs = P(("groups", "tp"), "dp")
    return jax.shard_map(shards, mesh=mesh, in_specs=in_specs, out_specs=out_specs, check_vma=False)
```

profile of v0, /device:TPU:0, one launch (start us, length us, event | category | flops | bytes accessed | tf_op | source)
XLA Modules:
  0.0 109.0 jit_solution(1227853281938794625)
XLA Ops:
  6.5 0.0 copy-start
  6.5 0.0 all-reduce.2.cloned.1.call-start
  6.5 0.7 fusion.11
  7.3 0.1 copy.8
  7.4 0.1 reduce-window.8
  7.4 0.0 copy-start.1
  7.4 0.1 add_reduce_fusion
  7.5 0.0 copy-done
  7.5 0.1 convolution_convert_fusion.3
  7.7 15.6 %all_gather.3 = bf16[64,1536]{1,0:T(8,128)(2,1)S(1)} all-gather(bf16[16,1536]{1,0:T(8,128)(2,1)S(1)} %convolution_convert_fusion.3), channel_id=1, replica_groups=mesh['groups'=2,'dp'=4,'tp'=4] {'tp'}, dimensions={0}, use_global_device_ids=true | all-gather | bytes 245760 | tf_op jit(solution)/shard_map/all_gather | solution.py:18
  23.3 6.9 %convolution_convert_fusion = bf16[64,4096]{1,0:T(8,128)(2,1)S(1)} fusion(bf16[64,1536]{1,0:T(8,128)(2,1)S(1)} %all_gather.3, bf16[1536,4096]{1,0:T(8,128)(2,1)} %param.8), kind=kOutput, calls=%fused_computation | convolution fusion | flops 805568512 | bytes 13303808 | tf_op jit(solution)/shard_map/dot_general | solution.py:22
  30.2 0.0 copy-done.1
  30.2 2.3 %convolution_convert_fusion.1 = bf16[64,4096]{1,0:T(8,128)(2,1)S(1)} fusion(bf16[64,1536]{1,0:T(8,128)(2,1)S(1)} %all_gather.3, bf16[1536,4096]{1,0:T(8,128)(2,1)S(1)} %copy-done.1), kind=kOutput, calls=%fused_computation.1 | convolution fusion | flops 805568512 | bytes 13303808 | tf_op jit(solution)/shard_map/dot_general | solution.py:19
  32.5 1.1 %pad_maximum_fusion = bf16[64,8192]{1,0:T(8,128)(2,1)} fusion(bf16[64,4096]{1,0:T(8,128)(2,1)S(1)} %convolution_convert_fusion, bf16[64,4096]{1,0:T(8,128)(2,1)S(1)} %convolution_convert_fusion.1), kind=kLoop, calls=%fused_computation.8 | loop fusion | flops 2097152 | bytes 2097152 | tf_op jit(solution)/shard_map/concatenate | solution.py:23
  33.6 0.0 all-reduce.2.cloned.1.call-update
  33.6 0.0 copy-start.2
  33.6 0.0 copy-start.3
  33.6 0.0 reduce-scatter.2.cloned.1.call-start
  33.7 37.7 %all-reduce.2.cloned.1.call-done = bf16[64,8192]{1,0:T(8,128)(2,1)} async-done(((bf16[64,8192]{1,0:T(8,128)(2,1)}), bf16[64,8192]{1,0:T(8,128)(2,1)}) %all-reduce.2.cloned.1.call-update) | async-done | bytes 1048592 | tf_op jit(solution)/shard_map/psum | solution.py:24
  71.3 1.4 %convert_element_type.44 = f32[64,8192]{1,0:T(8,128)S(1)} convert(bf16[64,8192]{1,0:T(8,128)(2,1)} %all-reduce.2.cloned.1.call-done) | non-fusion elementwise | flops 524288 | bytes 3145728 | tf_op jit(solution)/shard_map/convert_element_type | solution.py:24
  72.7 7.5 %convolution_convert_fusion.2 = bf16[64,1536]{1,0:T(8,128)(2,1)} fusion(bf16[4096,1536]{1,0:T(8,128)(2,1)} %param.9, f32[64,8192]{1,0:T(8,128)S(1)} %convert_element_type.44), kind=kOutput, calls=%fused_computation.2 | convolution fusion | flops 806977536 | bytes 14876672 | tf_op jit(solution)/shard_map/dot_general | solution.py:26
  80.2 0.0 reduce-scatter.2.cloned.1.call-update
  80.3 0.0 copy-done.2
  80.3 0.0 copy-done.3
  80.3 20.2 %reduce-scatter.2.cloned.1.call-done = bf16[16,1536]{1,0:T(8,128)(2,1)} async-done(((bf16[64,1536]{1,0:T(8,128)(2,1)}), bf16[16,1536]{1,0:T(8,128)(2,1)}) %reduce-scatter.2.cloned.1.call-update) | async-done | bytes 49168 | tf_op jit(solution)/shard_map/reduce_scatter | solution.py:29
  100.5 1.7 %fusion = bf16[32,1536]{1,0:T(8,128)(2,1)} fusion(bf16[16,1536]{1,0:T(8,128)(2,1)} %reduce-scatter.2.cloned.1.call-done, f32[32]{0:T(128)S(1)} %select_reduce_fusion, s32[32]{0:T(128)S(1)} %add_reduce_fusion, pred[32]{0:T(512)(128)(4,1)S(1)} %fusion.11), kind=kOutput, calls=%fused_computation.4 | convolution fusion | flops 1672192 | bytes 147744 | tf_op jit(solution)/shard_map/dot_general | solution.py:27
  (2 shorter events, 0.0 us)
Async XLA Ops:
  6.5 1.0 copy-start
  6.5 64.8 %all-reduce.2.cloned.1.call-start = ((), (), s32[]{:S(2)}) async-start(), calls=%async_computation.1 | async-start | bytes 2097152 | tf_op jit(solution)/shard_map/psum | solution.py:24
  7.4 22.7 %copy-start.1 = (bf16[1536,4096]{1,0:T(8,128)(2,1)S(1)}, bf16[1536,4096]{1,0:T(8,128)(2,1)}, u32[]{:S(2)}) copy-start(bf16[1536,4096]{1,0:T(8,128)(2,1)} %param.7) | copy-start | bytes 37748740
  33.6 46.7 %copy-start.2 = (s32[32,2]{0,1:T(2,128)S(1)}, s32[32,2]{0,1:T(2,128)}, u32[]{:S(2)}) copy-start(s32[32,2]{0,1:T(2,128)} %param.10) | copy-start | bytes 772
  33.6 46.7 %copy-start.3 = (f32[32,2]{0,1:T(2,128)S(1)}, f32[32,2]{0,1:T(2,128)}, u32[]{:S(2)}) copy-start(f32[32,2]{0,1:T(2,128)} %param.11) | copy-start | bytes 772
  33.6 66.9 %reduce-scatter.2.cloned.1.call-start = ((), (), s32[]{:S(2)}) async-start(), calls=%async_computation.2 | async-start | bytes 245760 | tf_op jit(solution)/shard_map/reduce_scatter | solution.py:29
Sparse Core Ops, SparseCore 0:
  33.7 37.5 all-reduce.1
  80.4 20.0 reduce-scatter.1
where the time goes:
time: 109 us
  waiting for transfers between devices  57.9 us (53%)
  matrix products  18.5 us (17%)
  blocking collectives  15.6 us (14%)
  between operations  13.5 us (12%)
  other arithmetic  3.39 us (3%)
    psum x1, waiting for transfers between devices, shards(): summed = lax.psum(gate_up, 'dp').astype(jnp.float32)  37.7 us
    reduce_scatter x1, waiting for transfers between devices, shards(): lax.psum_scatter(partial_value.astype(jnp.bfloat16), 'tp', scatter_dimens...  20.2 us
    all_gather x1, blocking collectives, shards(): row_block = lax.all_gather(packed, 'tp', axis=0, tiled=True)  15.6 us
    dot_general x1, matrix products, shards(): jnp.dot(hidden, down_weight, preferred_element_type=jnp.float32)  7.53 us
    dot_general x1, matrix products, shards(): jnp.dot(row_block, up_weight, preferred_element_type=jnp.float32)  6.87 us
    dot_general x1, matrix products, shards(): jnp.dot(row_block, gate_weight, preferred_element_type=jnp.float32)  2.3 us
  transfers between devices with their start and end apart: 2, of which 2 were waited for; matrix products, arithmetic and copies ran while one was open for 0% of the time, Pallas kernels for 0%

commit v1 on v0

v1 whole, which is shorter than its diff:
```python
import functools

import jax
import jax.numpy as jnp
from jax import lax
from jax.experimental import pallas as pl
from jax.experimental.pallas import tpu as pltpu
from jax.sharding import PartitionSpec as P

MOST = 16
F32 = jnp.float32
BF16 = jnp.bfloat16
PRIOR = 10000
WIDE = 512
GRANT = 8 * 1024 * 1024
VM = pl.BlockSpec(memory_space=pltpu.VMEM)


def call(body, outs, flops, nbytes, *args, scratch=()):
    return pl.pallas_call(
        body,
        out_shape=outs,
        in_specs=[VM] * len(args),
        out_specs=jax.tree.map(lambda _: VM, outs),
        scratch_shapes=scratch,
        compiler_params=pltpu.CompilerParams(vmem_limit_bytes=GRANT),
        cost_estimate=pl.CostEstimate(flops=flops, bytes_accessed=nbytes, transcendentals=0),
    )(*args)


def shape(dims, dtype):
    return jax.ShapeDtypeStruct(dims, dtype)


def in_vmem(array):
    return pltpu.with_memory_space_constraint(array, pltpu.VMEM)


def slots(ids_t):
    count = ids_t.shape[1]
    held = jnp.max(jnp.where(ids_t == 0, 1.0, 0.0), axis=0, keepdims=True)
    row = lax.broadcasted_iota(jnp.int32, (count, count), 0)
    col = lax.broadcasted_iota(jnp.int32, (count, count), 1)
    spread = jnp.broadcast_to(held, (count, count))
    rank = jnp.sum(jnp.where(col < row, spread, 0.0), axis=1, keepdims=True)
    routed = jnp.sum(jnp.where(col == row, spread, 0.0), axis=1, keepdims=True)
    slot = lax.broadcasted_iota(jnp.int32, (count, MOST), 1).astype(F32)
    return jnp.where((slot == rank) & (routed > 0.0), 1.0, 0.0)


def pack_body(ids_ref, tokens_ref, out_ref):
    one_hot = slots(ids_ref[...]).astype(BF16)
    out_ref[...] = lax.dot_general(
        one_hot, tokens_ref[...], (((0,), (0,)), ((), ())), preferred_element_type=F32
    ).astype(BF16)


def gate_up_body(n_tp, *refs):
    blocks = refs[:n_tp]
    gate_ref, up_ref, keep_ref, send_ref, scratch = refs[n_tp:]
    place = lax.axis_index("dp") ^ lax.axis_index("tp")
    for q, block in enumerate(blocks):
        spot = place ^ q
        spot = (spot % 2) * 2 + spot // 2
        scratch[pl.ds(pl.multiple_of(spot * MOST, MOST), MOST), :] = block[...]
    rows = scratch[...]
    half = rows.shape[0] // 2
    width = gate_ref.shape[1]
    step = min(WIDE, width)
    for k, weight in enumerate((gate_ref, up_ref)):

        def chunk(i, _, k=k, weight=weight):
            at = pl.ds(pl.multiple_of(i * step, step), step)
            part = jnp.dot(rows, weight[:, at], preferred_element_type=F32).astype(BF16)
            keep_ref[k, :, at] = part[:half]
            send_ref[k, :, at] = part[half:]
            return 0

        lax.fori_loop(0, width // step, chunk, 0)


def fold_body(keep_ref, got_ref, own_ref, send_ref):
    half = keep_ref.shape[1] // 2
    own_ref[...] = keep_ref[:, :half].astype(F32) + got_ref[:, :half].astype(F32)
    send_ref[...] = (keep_ref[:, half:].astype(F32) + got_ref[:, half:].astype(F32)).astype(BF16)


def hidden_body(own_ref, got_ref, out_ref):
    total = own_ref[...] + got_ref[...].astype(F32)
    gate, up = total[0], total[1]
    out_ref[...] = (gate / (1.0 + jnp.exp(-gate)) * up).astype(BF16)


def down_body(n_tp, *refs):
    weight_ref, own_ref = refs[4:6]
    sends, scratch = refs[6 : 5 + n_tp], refs[5 + n_tp]
    hidden = jnp.concatenate([ref[...] for ref in refs[:4]], axis=0)
    width = weight_ref.shape[1]
    step = min(WIDE, width)

    def chunk(i, _):
        at = pl.ds(pl.multiple_of(i * step, step), step)
        scratch[:, at] = jnp.dot(hidden, weight_ref[:, at], preferred_element_type=F32)
        return 0

    lax.fori_loop(0, width // step, chunk, 0)
    place = lax.axis_index("dp") ^ lax.axis_index("tp")
    for q in range(n_tp):
        block = scratch[pl.ds(pl.multiple_of((place ^ q) * MOST, MOST), MOST), :]
        if q == 0:
            own_ref[...] = block
        else:
            sends[q - 1][...] = block.astype(BF16)


def final_body(ids_ref, route_ref, own_ref, *refs):
    out_ref = refs[-1]
    total = own_ref[...]
    for got in refs[:-1]:
        total = total + got[...].astype(F32)
    ids = ids_ref[...]
    count = ids.shape[1]
    held = jnp.sum(jnp.where(ids == 0, route_ref[...], 0.0), axis=0, keepdims=True)
    row = lax.broadcasted_iota(jnp.int32, (count, count), 0)
    col = lax.broadcasted_iota(jnp.int32, (count, count), 1)
    combine = jnp.sum(
        jnp.where(col == row, jnp.broadcast_to(held, (count, count)), 0.0), axis=1, keepdims=True
    )
    spread = jnp.dot(
        slots(ids), total, precision=lax.Precision.HIGHEST, preferred_element_type=F32
    )
    out_ref[...] = (combine * spread).astype(BF16)


def swap(value, axis, size, mask):
    return lax.ppermute(value, axis, [(i, i ^ mask) for i in range(size)])


def direct(n_dp, n_tp, tokens, gate_weight, up_weight, down_weight, expert_ids, route_weights):
    ids_t, route_t = expert_ids.T, route_weights.T
    model, width = gate_weight.shape
    out_width = down_weight.shape[1]
    total = MOST * n_tp
    gate_weight, up_weight, down_weight = map(in_vmem, (gate_weight, up_weight, down_weight))
    packed = call(
        pack_body, shape((MOST, model), BF16), PRIOR * total * model * width, PRIOR * model * width, ids_t, tokens
    )
    got = [packed] + [swap(packed, "tp", n_tp, q) for q in range(1, n_tp)]
    keep, send = call(
        functools.partial(gate_up_body, n_tp),
        [shape((2, total // 2, width), BF16)] * 2,
        4 * total * model * width,
        4 * model * width,
        *got,
        gate_weight,
        up_weight,
        scratch=[pltpu.VMEM((total, model), BF16)],
    )
    got = swap(send, "dp", n_dp, 1)
    own, send = call(
        fold_body,
        [shape((2, total // 4, width), F32), shape((2, total // 4, width), BF16)],
        total * width,
        6 * total * width,
        keep,
        got,
    )
    got = swap(send, "dp", n_dp, 2)
    hidden = call(
        hidden_body, shape((total // 4, width), BF16), total * width, 3 * total * width, own, got
    )
    across = swap(hidden, "dp", n_dp, 2)
    beside = swap(hidden, "dp", n_dp, 1)
    corner = swap(across, "dp", n_dp, 1)
    own, *sends = call(
        functools.partial(down_body, n_tp),
        [shape((MOST, out_width), F32)] + [shape((MOST, out_width), BF16)] * (n_tp - 1),
        2 * total * width * out_width,
        2 * width * out_width,
        hidden,
        beside,
        across,
        corner,
        down_weight,
        scratch=[pltpu.VMEM((total, out_width), F32)],
    )
    got = [swap(s, "tp", n_tp, q + 1) for q, s in enumerate(sends)]
    return call(
        final_body,
        shape((tokens.shape[0], out_width), BF16),
        2 * tokens.size,
        4 * tokens.size,
        ids_t,
        route_t,
        own,
        *got,
    )


def general(tokens, gate_weight, up_weight, down_weight, expert_ids, route_weights):
    held_mask = expert_ids == 0
    combine = jnp.sum(jnp.where(held_mask, route_weights, jnp.zeros_like(route_weights)), axis=1)
    hidden_width = gate_weight.shape[1]
    routed = jnp.any(held_mask, axis=1)
    slot_rank = jnp.cumsum(routed.astype(jnp.int32)) - 1
    slot_ids = jnp.arange(MOST, dtype=jnp.int32)
    dispatch = ((slot_rank[None, :] == slot_ids[:, None]) & routed[None, :]).astype(BF16)
    packed = jnp.dot(dispatch, tokens, preferred_element_type=F32).astype(BF16)
    row_block = lax.all_gather(packed, "tp", axis=0, tiled=True)
    gate_part = jnp.dot(row_block, gate_weight, preferred_element_type=F32).astype(BF16)
    up_part = jnp.dot(row_block, up_weight, preferred_element_type=F32).astype(BF16)
    gate_up = jnp.concatenate([gate_part, up_part], axis=1)
    summed = lax.psum(gate_up, "dp").astype(F32)
    hidden = (jax.nn.silu(summed[:, :hidden_width]) * summed[:, hidden_width:]).astype(BF16)
    partial_value = jnp.dot(hidden, down_weight, preferred_element_type=F32)
    result = jnp.dot(
        dispatch.T.astype(F32),
        lax.psum_scatter(
            partial_value.astype(BF16), "tp", scatter_dimension=0, tiled=True
        ).astype(F32),
        precision=lax.Precision.HIGHEST,
    )
    return (combine[:, None] * result).astype(BF16)


def solution(mesh):
    n_dp, n_tp = mesh.shape["dp"], mesh.shape["tp"]
    in_specs = (
        P(("groups", "tp"), "dp"),
        P("dp", "tp"),
        P("dp", "tp"),
        P("tp", "dp"),
        P(("groups", "tp"), None),
        P(("groups", "tp"), None),
    )
    out_specs = P(("groups", "tp"), "dp")
    body = functools.partial(direct, n_dp, n_tp) if n_dp == n_tp == 4 else general
    return jax.shard_map(body, mesh=mesh, in_specs=in_specs, out_specs=out_specs, check_vma=False)
```

time: 109 us -> 48.5 us (0.44)
  waiting for transfers between devices: 57.9 us -> 22.8 us
  matrix products: 18.5 us -> 0 us
  blocking collectives: 15.6 us -> 0 us
  between operations: 13.5 us -> 0.07 us
  starting transfers between devices: 0.04 us -> 13.4 us
  Pallas kernels: 0 us -> 10.5 us
  other arithmetic: 3.39 us -> 0 us
  local copies, waits for them, and re-layouts: 0.11 us -> 1.6 us
    psum x1 -> x0, waiting for transfers between devices: 37.7 us -> none  [shards(): summed = lax.psum(gate_up, 'dp').astype(jnp.float32)]
    ppermute x0 -> x11, waiting for transfers between devices: none -> 22.8 us  [swap(): return lax.ppermute(value, axis, [(i, i ^ mask) for i in range(size)])]
    reduce_scatter x1 -> x0, waiting for transfers between devices: 20.2 us -> none  [shards(): lax.psum_scatter(partial_value.astype(jnp.bfloat16), 'tp', scatter_dimens...]
    dot_general x5 -> x0, matrix products: 18.5 us -> none  [the longest x1 7.53 us: shards(): jnp.dot(hidden, down_weight, preferred_element_type=jnp.float32)]
    all_gather x1 -> x0, blocking collectives: 15.6 us -> none  [shards(): row_block = lax.all_gather(packed, 'tp', axis=0, tiled=True)]
    ppermute x0 -> x11, starting transfers between devices: none -> 13.4 us  [swap(): return lax.ppermute(value, axis, [(i, i ^ mask) for i in range(size)])]
    pallas_call x0 -> x6, Pallas kernels: none -> 10.5 us  [call(): pl.pallas_call(body, out_shape=outs, in_specs=[VM] * len(args), out_specs...]
    unnamed x8 -> x14, local copies, waits for them, and re-layouts: 0.02 us -> 1.6 us
  transfers between devices with their start and end apart: 2 -> 11, of which waited for: 2 -> 8; matrix products, arithmetic and copies ran while one was open for 0% -> 0% of each run, Pallas kernels for 0% -> 0%
where the time goes in v1:
time: 48.5 us; the launch traced here: 48.4 us
  waiting for transfers between devices  22.8 us (47%)
  starting transfers between devices  13.4 us (28%)
  Pallas kernels  10.5 us (22%)
  local copies, waits for them, and re-layouts  1.6 us (3%)
    ppermute x11, waiting for transfers between devices, swap(): return lax.ppermute(value, axis, [(i, i ^ mask) for i in range(size)])  22.8 us
    ppermute x11, starting transfers between devices, swap(): return lax.ppermute(value, axis, [(i, i ^ mask) for i in range(size)])  13.4 us
    pallas_call x6, Pallas kernels, call(): pl.pallas_call(body, out_shape=outs, in_specs=[VM] * len(args), out_specs...  10.5 us
    unnamed x14, local copies, waits for them, and re-layouts  1.6 us
  transfers between devices with their start and end apart: 11, of which 8 were waited for; matrix products, arithmetic and copies ran while one was open for 0% of the time, Pallas kernels for 0%

profile of v1, /device:TPU:0, one launch (start us, length us, event | category | flops | bytes accessed | tf_op | source)
XLA Modules:
  0.0 48.4 jit_solution(12389797261551630816)
XLA Ops:
  0.0 0.0 copy-start.3
  0.0 0.7 %copy-done.3 = s32[32,2]{0,1:T(2,128)S(1)} copy-done((s32[32,2]{0,1:T(2,128)S(1)}, s32[32,2]{0,1:T(2,128)}, u32[]{:S(2)}) %copy-start.3) | copy-done | bytes 280
  0.7 0.0 copy-start.6
  0.7 0.9 %copy-done.6 = bf16[32,1536]{1,0:T(8,128)(2,1)S(1)} copy-done((bf16[32,1536]{1,0:T(8,128)(2,1)S(1)}, bf16[32,1536]{1,0:T(8,128)(2,1)}, u32[]{:S(2)}) %copy-start.6) | copy-done | bytes 98328
  1.6 0.0 copy-start
  1.6 0.0 copy-start.1
  1.6 0.3 shard_map.64.refs_0_
  1.8 0.0 copy-start.2
  1.9 5.1 %collective-permute-start.2 = (bf16[16,1536]{1,0:T(8,128)(2,1)S(1)}, bf16[16,1536]{1,0:T(8,128)(2,1)S(1)}, u32[]{:S(2)}, u32[]{:S(2)}) collective-permute-start(bf16[16,1536]{1,0:T(8,128)(2,1)S(1)} %shard_map.64.refs_0_), channel_id=1, source_target_pairs={{0,3},{1,2},{2,1},{3,0},{4,7},{5,6},{6,5},{7,4},{8,11},{9,10},{10,... | collective-permute-start | bytes 147464 | tf_op jit(solution)/shard_map/ppermute | solution.py:136
  7.0 0.0 collective-permute-start.1
  7.0 0.6 %collective-permute-start = (bf16[16,1536]{1,0:T(8,128)(2,1)S(1)}, bf16[16,1536]{1,0:T(8,128)(2,1)S(1)}, u32[]{:S(2)}, u32[]{:S(2)}) collective-permute-start(bf16[16,1536]{1,0:T(8,128)(2,1)S(1)} %shard_map.64.refs_0_), channel_id=1, source_target_pairs={{0,1},{1,0},{2,3},{3,2},{4,5},{5,4},{6,7},{7,6},{8,9},{9,8},{10,11... | collective-permute-start | bytes 147464 | tf_op jit(solution)/shard_map/ppermute | solution.py:136
  7.6 1.5 %collective-permute-done.2.refs_3_ = bf16[16,1536]{1,0:T(8,128)(2,1)S(1)} collective-permute-done((bf16[16,1536]{1,0:T(8,128)(2,1)S(1)}, bf16[16,1536]{1,0:T(8,128)(2,1)S(1)}, u32[]{:S(2)}, u32[]{:S(2)}) %collective-permute-start.2) | collective-permute-done | bytes 49184 | tf_op jit(solution)/shard_map/ppermute | solution.py:136
  9.1 2.9 %collective-permute-done.1.refs_2_ = bf16[16,1536]{1,0:T(8,128)(2,1)S(1)} collective-permute-done((bf16[16,1536]{1,0:T(8,128)(2,1)S(1)}, bf16[16,1536]{1,0:T(8,128)(2,1)S(1)}, u32[]{:S(2)}, u32[]{:S(2)}) %collective-permute-start.1) | collective-permute-done | bytes 49184 | tf_op jit(solution)/shard_map/ppermute | solution.py:136
  12.0 0.0 collective-permute-done.refs_1_
  12.0 0.0 copy-done
  12.0 0.0 copy-done.1
  12.0 6.4 %shard_map.65 = (bf16[2,32,4096]{2,1,0:T(8,128)(2,1)S(1)}, bf16[2,32,4096]{2,1,0:T(8,128)(2,1)S(1)}) custom-call(bf16[16,1536]{1,0:T(8,128)(2,1)S(1)} %shard_map.64.refs_0_, bf16[16,1536]{1,0:T(8,128)(2,1)S(1)} %collective-permute-done.refs_1_, bf16[16,1536]{1,0:T(8,128)(2,1)S(1)} %collective-permute-done.1.refs_2_, ...), custom_call_target="tpu_custom_call" | custom-call | flops 1610612736 | bytes 25165824 | tf_op jit(solution)/shard_map/pallas_call | solution.py:20
  18.4 0.0 copy-start.4
  18.4 0.0 copy-start.5
  18.4 0.1 collective-permute-start.3
  18.5 1.9 %collective-permute-done.3.got_ref = bf16[2,32,4096]{2,1,0:T(8,128)(2,1)S(1)} collective-permute-done((bf16[2,32,4096]{2,1,0:T(8,128)(2,1)S(1)}, bf16[2,32,4096]{2,1,0:T(8,128)(2,1)S(1)}, u32[]{:S(2)}, u32[]{:S(2)}) %collective-permute-start.3) | collective-permute-done | bytes 524320 | tf_op jit(solution)/shard_map/ppermute | solution.py:136
  20.4 0.1 shard_map.66
  20.5 1.6 %collective-permute-start.4 = (bf16[2,16,4096]{2,1,0:T(8,128)(2,1)S(1)}, bf16[2,16,4096]{2,1,0:T(8,128)(2,1)S(1)}, u32[]{:S(2)}, u32[]{:S(2)}) collective-permute-start(bf16[2,16,4096]{2,1,0:T(8,128)(2,1)S(1)} %get-tuple-element.16), channel_id=1, source_target_pairs={{0,8},{4,12},{8,0},{12,4},{1,9},{5,13},{9,1},{13,5},{2,10},{6,14},... | collective-permute-start | bytes 786440 | tf_op jit(solution)/shard_map/ppermute | solution.py:136
  22.1 6.9 %collective-permute-done.4.got_ref = bf16[2,16,4096]{2,1,0:T(8,128)(2,1)S(1)} collective-permute-done((bf16[2,16,4096]{2,1,0:T(8,128)(2,1)S(1)}, bf16[2,16,4096]{2,1,0:T(8,128)(2,1)S(1)}, u32[]{:S(2)}, u32[]{:S(2)}) %collective-permute-start.4) | collective-permute-done | bytes 262176 | tf_op jit(solution)/shard_map/ppermute | solution.py:136
  28.9 0.1 shard_map.67.refs_0_
  29.0 1.6 %collective-permute-start.6 = (bf16[16,4096]{1,0:T(8,128)(2,1)S(1)}, bf16[16,4096]{1,0:T(8,128)(2,1)S(1)}, u32[]{:S(2)}, u32[]{:S(2)}) collective-permute-start(bf16[16,4096]{1,0:T(8,128)(2,1)S(1)} %shard_map.67.refs_0_), channel_id=1, source_target_pairs={{0,8},{4,12},{8,0},{12,4},{1,9},{5,13},{9,1},{13,5},{2,10},{6,14},... | collective-permute-start | bytes 393224 | tf_op jit(solution)/shard_map/ppermute | solution.py:136
  30.6 0.0 collective-permute-start.5
  30.6 3.5 %collective-permute-done.6.refs_2_ = bf16[16,4096]{1,0:T(8,128)(2,1)S(1)} collective-permute-done((bf16[16,4096]{1,0:T(8,128)(2,1)S(1)}, bf16[16,4096]{1,0:T(8,128)(2,1)S(1)}, u32[]{:S(2)}, u32[]{:S(2)}) %collective-permute-start.6) | collective-permute-done | bytes 131104 | tf_op jit(solution)/shard_map/ppermute | solution.py:136
  34.1 0.0 collective-permute-start.7
  34.1 0.0 collective-permute-done.5.refs_1_
  34.1 1.3 %collective-permute-done.7.refs_3_ = bf16[16,4096]{1,0:T(8,128)(2,1)S(1)} collective-permute-done((bf16[16,4096]{1,0:T(8,128)(2,1)S(1)}, bf16[16,4096]{1,0:T(8,128)(2,1)S(1)}, u32[]{:S(2)}, u32[]{:S(2)}) %collective-permute-start.7) | collective-permute-done | bytes 131104 | tf_op jit(solution)/shard_map/ppermute | solution.py:136
  35.4 0.0 copy-done.2
  35.4 2.6 %shard_map.68 = (f32[16,1536]{1,0:T(8,128)S(1)}, bf16[16,1536]{1,0:T(8,128)(2,1)S(1)}, bf16[16,1536]{1,0:T(8,128)(2,1)S(1)}, bf16[16,1536]{1,0:T(8,128)(2,1)S(1)}) custom-call(bf16[16,4096]{1,0:T(8,128)(2,1)S(1)} %shard_map.67.refs_0_, bf16[16,4096]{1,0:T(8,128)(2,1)S(1)} %collective-permute-done.5.refs_1_, ...), custom_call_target="tpu_custom_call" | custom-call | flops 805306368 | bytes 12582912 | tf_op jit(solution)/shard_map/pallas_call | solution.py:20
  38.0 0.8 %collective-permute-start.8 = (bf16[16,1536]{1,0:T(8,128)(2,1)S(1)}, bf16[16,1536]{1,0:T(8,128)(2,1)S(1)}, u32[]{:S(2)}, u32[]{:S(2)}) collective-permute-start(bf16[16,1536]{1,0:T(8,128)(2,1)S(1)} %get-tuple-element.18), channel_id=1, source_target_pairs={{0,1},{1,0},{2,3},{3,2},{4,5},{5,4},{6,7},{7,6},{8,9},{9,8},{10,11... | collective-permute-start | bytes 147464 | tf_op jit(solution)/shard_map/ppermute | solution.py:136
  38.8 2.6 %collective-permute-start.9 = (bf16[16,1536]{1,0:T(8,128)(2,1)S(1)}, bf16[16,1536]{1,0:T(8,128)(2,1)S(1)}, u32[]{:S(2)}, u32[]{:S(2)}) collective-permute-start(bf16[16,1536]{1,0:T(8,128)(2,1)S(1)} %get-tuple-element.19), channel_id=1, source_target_pairs={{0,2},{1,3},{2,0},{3,1},{4,6},{5,7},{6,4},{7,5},{8,10},{9,11},{10,... | collective-permute-start | bytes 147464 | tf_op jit(solution)/shard_map/ppermute | solution.py:136
  41.4 1.0 %collective-permute-start.10 = (bf16[16,1536]{1,0:T(8,128)(2,1)S(1)}, bf16[16,1536]{1,0:T(8,128)(2,1)S(1)}, u32[]{:S(2)}, u32[]{:S(2)}) collective-permute-start(bf16[16,1536]{1,0:T(8,128)(2,1)S(1)} %get-tuple-element.20), channel_id=1, source_target_pairs={{0,3},{1,2},{2,1},{3,0},{4,7},{5,6},{6,5},{7,4},{8,11},{9,10},{10,... | collective-permute-start | bytes 147464 | tf_op jit(solution)/shard_map/ppermute | solution.py:136
  42.4 0.0 collective-permute-done.8.refs_0_
  42.4 2.4 %collective-permute-done.9.refs_1_ = bf16[16,1536]{1,0:T(8,128)(2,1)S(1)} collective-permute-done((bf16[16,1536]{1,0:T(8,128)(2,1)S(1)}, bf16[16,1536]{1,0:T(8,128)(2,1)S(1)}, u32[]{:S(2)}, u32[]{:S(2)}) %collective-permute-start.9) | collective-permute-done | bytes 49184 | tf_op jit(solution)/shard_map/ppermute | solution.py:136
  44.9 2.4 %collective-permute-done.10.refs_2_ = bf16[16,1536]{1,0:T(8,128)(2,1)S(1)} collective-permute-done((bf16[16,1536]{1,0:T(8,128)(2,1)S(1)}, bf16[16,1536]{1,0:T(8,128)(2,1)S(1)}, u32[]{:S(2)}, u32[]{:S(2)}) %collective-permute-start.10) | collective-permute-done | bytes 49184 | tf_op jit(solution)/shard_map/ppermute | solution.py:136
  47.3 0.0 copy-done.4
  47.3 0.0 copy-done.5
  47.3 1.0 %shard_map.69 = bf16[32,1536]{1,0:T(8,128)(2,1)} custom-call(s32[2,32]{1,0:T(2,128)S(1)} %bitcast.3, f32[2,32]{1,0:T(2,128)S(1)} %bitcast.4, f32[16,1536]{1,0:T(8,128)S(1)} %get-tuple-element.17.own_ref, bf16[16,1536]{1,0:T(8,128)(2,1)S(1)} %collective-permute-done.8.refs_0_, bf16[16,1536]{1,0:T(8,128)(2,1)S(1)} %collective-permute-done.9.refs_1_, ...), custom_call_target="tpu_custom_call" | custom-call | flops 98304 | bytes 196608 | tf_op jit(solution)/shard_map/pallas_call | solution.py:20
Async XLA Ops:
  0.0 0.7 %copy-start.3 = (s32[32,2]{0,1:T(2,128)S(1)}, s32[32,2]{0,1:T(2,128)}, u32[]{:S(2)}) copy-start(s32[32,2]{0,1:T(2,128)} %param.10) | copy-start | bytes 772
  0.7 0.9 %copy-start.6 = (bf16[32,1536]{1,0:T(8,128)(2,1)S(1)}, bf16[32,1536]{1,0:T(8,128)(2,1)}, u32[]{:S(2)}) copy-start(bf16[32,1536]{1,0:T(8,128)(2,1)} %tokens_ref.1) | copy-start | bytes 294916
  1.6 10.4 %copy-start = (bf16[1536,4096]{1,0:T(8,128)(2,1)S(1)}, bf16[1536,4096]{1,0:T(8,128)(2,1)}, u32[]{:S(2)}) copy-start(bf16[1536,4096]{1,0:T(8,128)(2,1)} %refs_4_.2) | copy-start | bytes 37748740
  1.6 10.4 %copy-start.1 = (bf16[1536,4096]{1,0:T(8,128)(2,1)S(1)}, bf16[1536,4096]{1,0:T(8,128)(2,1)}, u32[]{:S(2)}) copy-start(bf16[1536,4096]{1,0:T(8,128)(2,1)} %refs_5_.1) | copy-start | bytes 37748740
  1.8 33.6 %copy-start.2 = (bf16[4096,1536]{1,0:T(8,128)(2,1)S(1)}, bf16[4096,1536]{1,0:T(8,128)(2,1)}, u32[]{:S(2)}) copy-start(bf16[4096,1536]{1,0:T(8,128)(2,1)} %refs_4_.3) | copy-start | bytes 37748740
  1.9 7.3 %collective-permute-start.2 = (bf16[16,1536]{1,0:T(8,128)(2,1)S(1)}, bf16[16,1536]{1,0:T(8,128)(2,1)S(1)}, u32[]{:S(2)}, u32[]{:S(2)}) collective-permute-start(bf16[16,1536]{1,0:T(8,128)(2,1)S(1)} %shard_map.64.refs_0_), channel_id=1, source_target_pairs={{0,3},{1,2},{2,1},{3,0},{4,7},{5,6},{6,5},{7,4},{8,11},{9,10},{10,... | collective-permute-start | bytes 147464 | tf_op jit(solution)/shard_map/ppermute | solution.py:136
  7.0 5.0 %collective-permute-start.1 = (bf16[16,1536]{1,0:T(8,128)(2,1)S(1)}, bf16[16,1536]{1,0:T(8,128)(2,1)S(1)}, u32[]{:S(2)}, u32[]{:S(2)}) collective-permute-start(bf16[16,1536]{1,0:T(8,128)(2,1)S(1)} %shard_map.64.refs_0_), channel_id=1, source_target_pairs={{0,2},{1,3},{2,0},{3,1},{4,6},{5,7},{6,4},{7,5},{8,10},{9,11},{10,... | collective-permute-start | bytes 147464 | tf_op jit(solution)/shard_map/ppermute | solution.py:136
  7.0 5.0 %collective-permute-start = (bf16[16,1536]{1,0:T(8,128)(2,1)S(1)}, bf16[16,1536]{1,0:T(8,128)(2,1)S(1)}, u32[]{:S(2)}, u32[]{:S(2)}) collective-permute-start(bf16[16,1536]{1,0:T(8,128)(2,1)S(1)} %shard_map.64.refs_0_), channel_id=1, source_target_pairs={{0,1},{1,0},{2,3},{3,2},{4,5},{5,4},{6,7},{7,6},{8,9},{9,8},{10,11... | collective-permute-start | bytes 147464 | tf_op jit(solution)/shard_map/ppermute | solution.py:136
  18.4 28.9 %copy-start.4 = (s32[32,2]{0,1:T(2,128)S(1)}, s32[32,2]{0,1:T(2,128)}, u32[]{:S(2)}) copy-start(s32[32,2]{0,1:T(2,128)} %param.10) | copy-start | bytes 772
  18.4 28.9 %copy-start.5 = (f32[32,2]{0,1:T(2,128)S(1)}, f32[32,2]{0,1:T(2,128)}, u32[]{:S(2)}) copy-start(f32[32,2]{0,1:T(2,128)} %param.11) | copy-start | bytes 772
  18.4 2.0 %collective-permute-start.3 = (bf16[2,32,4096]{2,1,0:T(8,128)(2,1)S(1)}, bf16[2,32,4096]{2,1,0:T(8,128)(2,1)S(1)}, u32[]{:S(2)}, u32[]{:S(2)}) collective-permute-start(bf16[2,32,4096]{2,1,0:T(8,128)(2,1)S(1)} %get-tuple-element.14), channel_id=1, source_target_pairs={{0,4},{4,0},{8,12},{12,8},{1,5},{5,1},{9,13},{13,9},{2,6},{6,2},{1... | collective-permute-start | bytes 1572872 | tf_op jit(solution)/shard_map/ppermute | solution.py:136
  20.5 8.4 %collective-permute-start.4 = (bf16[2,16,4096]{2,1,0:T(8,128)(2,1)S(1)}, bf16[2,16,4096]{2,1,0:T(8,128)(2,1)S(1)}, u32[]{:S(2)}, u32[]{:S(2)}) collective-permute-start(bf16[2,16,4096]{2,1,0:T(8,128)(2,1)S(1)} %get-tuple-element.16), channel_id=1, source_target_pairs={{0,8},{4,12},{8,0},{12,4},{1,9},{5,13},{9,1},{13,5},{2,10},{6,14},... | collective-permute-start | bytes 786440 | tf_op jit(solution)/shard_map/ppermute | solution.py:136
  29.0 5.0 %collective-permute-start.6 = (bf16[16,4096]{1,0:T(8,128)(2,1)S(1)}, bf16[16,4096]{1,0:T(8,128)(2,1)S(1)}, u32[]{:S(2)}, u32[]{:S(2)}) collective-permute-start(bf16[16,4096]{1,0:T(8,128)(2,1)S(1)} %shard_map.67.refs_0_), channel_id=1, source_target_pairs={{0,8},{4,12},{8,0},{12,4},{1,9},{5,13},{9,1},{13,5},{2,10},{6,14},... | collective-permute-start | bytes 393224 | tf_op jit(solution)/shard_map/ppermute | solution.py:136
  30.6 3.5 %collective-permute-start.5 = (bf16[16,4096]{1,0:T(8,128)(2,1)S(1)}, bf16[16,4096]{1,0:T(8,128)(2,1)S(1)}, u32[]{:S(2)}, u32[]{:S(2)}) collective-permute-start(bf16[16,4096]{1,0:T(8,128)(2,1)S(1)} %shard_map.67.refs_0_), channel_id=1, source_target_pairs={{0,4},{4,0},{8,12},{12,8},{1,5},{5,1},{9,13},{13,9},{2,6},{6,2},{1... | collective-permute-start | bytes 393224 | tf_op jit(solution)/shard_map/ppermute | solution.py:136
  34.1 1.3 %collective-permute-start.7 = (bf16[16,4096]{1,0:T(8,128)(2,1)S(1)}, bf16[16,4096]{1,0:T(8,128)(2,1)S(1)}, u32[]{:S(2)}, u32[]{:S(2)}) collective-permute-start(bf16[16,4096]{1,0:T(8,128)(2,1)S(1)} %collective-permute-done.6.refs_2_), channel_id=1, source_target_pairs={{0,4},{4,0},{8,12},{12,8},{1,5},{5,1},{9,13},{13,9},{2,6},{6,2},{1... | collective-permute-start | bytes 393224 | tf_op jit(solution)/shard_map/ppermute | solution.py:136
  38.0 4.5 %collective-permute-start.8 = (bf16[16,1536]{1,0:T(8,128)(2,1)S(1)}, bf16[16,1536]{1,0:T(8,128)(2,1)S(1)}, u32[]{:S(2)}, u32[]{:S(2)}) collective-permute-start(bf16[16,1536]{1,0:T(8,128)(2,1)S(1)} %get-tuple-element.18), channel_id=1, source_target_pairs={{0,1},{1,0},{2,3},{3,2},{4,5},{5,4},{6,7},{7,6},{8,9},{9,8},{10,11... | collective-permute-start | bytes 147464 | tf_op jit(solution)/shard_map/ppermute | solution.py:136
  38.8 6.0 %collective-permute-start.9 = (bf16[16,1536]{1,0:T(8,128)(2,1)S(1)}, bf16[16,1536]{1,0:T(8,128)(2,1)S(1)}, u32[]{:S(2)}, u32[]{:S(2)}) collective-permute-start(bf16[16,1536]{1,0:T(8,128)(2,1)S(1)} %get-tuple-element.19), channel_id=1, source_target_pairs={{0,2},{1,3},{2,0},{3,1},{4,6},{5,7},{6,4},{7,5},{8,10},{9,11},{10,... | collective-permute-start | bytes 147464 | tf_op jit(solution)/shard_map/ppermute | solution.py:136
  41.4 5.9 %collective-permute-start.10 = (bf16[16,1536]{1,0:T(8,128)(2,1)S(1)}, bf16[16,1536]{1,0:T(8,128)(2,1)S(1)}, u32[]{:S(2)}, u32[]{:S(2)}) collective-permute-start(bf16[16,1536]{1,0:T(8,128)(2,1)S(1)} %get-tuple-element.20), channel_id=1, source_target_pairs={{0,3},{1,2},{2,1},{3,0},{4,7},{5,6},{6,5},{7,4},{8,11},{9,10},{10,... | collective-permute-start | bytes 147464 | tf_op jit(solution)/shard_map/ppermute | solution.py:136
